TPU v7x, 32 devices: a whole 2x2x4 slice. The times are simulated.
32 devices in a mesh: fsdp: 4 (over z), context: 8 (over y, x, core).
Axes of the slice: x: 2, y: 2, z: 4, core: 2. Of those that a mesh axis runs over, the one named last changes fastest.
Arguments:
- block_input: bfloat16 [4, 1024, 1536], P('fsdp', 'context'), may hold values from -15 to 15
- cotangent: bfloat16 [4, 1024, 1536], P('fsdp', 'context'), may hold values from -6 to 6
- documents: int32 [4, 1024], P('fsdp', 'context'), may hold values from 0 to 7, as said below
- attn_weights: float32 [4608, 1536], P(('fsdp', 'context')), may hold values from -1.5 to 1.5
- ffn_weights: float32 [12288, 1536], P(('fsdp', 'context')), may hold values from -0.36 to 0.36
- norm_gains: float32 [2, 1536], replicated, may hold values from -0.5 to 0.5
- attn_moments: float32 [2, 4608, 1536], P(None, ('fsdp', 'context')), may hold values from -0.8 to 0.8, as said below
- ffn_moments: float32 [2, 12288, 1536], P(None, ('fsdp', 'context')), may hold values from -0.8 to 0.8, as said below
- gain_moments: float32 [2, 2, 1536], P(None, None, ('fsdp', 'context')), may hold values from -0.8 to 0.8, as said below
Outputs:
- block_output: float32 [4, 1024, 1536], P('fsdp', 'context')
- input_grad: float32 [4, 1024, 1536], P('fsdp', 'context')
- attn_grad: float32 [4608, 1536], P(('fsdp', 'context'))
- ffn_grad: float32 [12288, 1536], P(('fsdp', 'context'))
- gain_grad: float32 [2, 1536], P(None, ('fsdp', 'context'))
- new_attn_weights: float32 [4608, 1536], P(('fsdp', 'context'))
- new_ffn_weights: float32 [12288, 1536], P(('fsdp', 'context'))
- new_norm_gains: float32 [2, 1536], P(None, ('fsdp', 'context'))
- new_attn_moments: float32 [2, 4608, 1536], P(None, ('fsdp', 'context'))
- new_ffn_moments: float32 [2, 12288, 1536], P(None, ('fsdp', 'context'))
- new_gain_moments: float32 [2, 2, 1536], P(None, None, ('fsdp', 'context'))
Inputs may be any that keep to these rules, and one draw needn't show every extreme that they name: Segment numbers never fall along a sequence and start at 0; each sequence holds 8 documents of 50 to 640 tokens, one of exactly 640. `attn_moments`: entry 1 along the first dimension is positive. `ffn_moments`: entry 1 along the first dimension is positive. `gain_moments`: entry 1 along the first dimension is positive.
All inputs are finite; a program needn't handle non-finite values.
Results may differ from a plain program's by a relative error of at most 0.015.
Values may be sent and summed in bfloat16 or wider, within the bound.
A program may use at most 448 MiB of HBM per device.

v0:
```python
import math
import jax
import jax.numpy as jnp
from jax import lax
from jax.sharding import PartitionSpec as P

FF = 4096
QUERY_HEADS = 16
KEY_VALUE_HEADS = 8
HEAD_SIZE = 96
STEP = 3
NORM_EPS = 1e-05
ROPE_THETA = 100000.0
BETA_ONE = 0.9
BETA_TWO = 0.95
ADAM_EPS = 1e-08
LEARN_RATE = 0.02
WEIGHT_DECAY = 0.1


def product_transposed(left_matrix, right_matrix):
    return lax.dot_general(
        left_matrix, right_matrix, (((1,), (1,)), ((), ())), preferred_element_type=jnp.float32
    )


def transposed_times(left_matrix, right_matrix):
    return lax.dot_general(
        left_matrix, right_matrix, (((0,), (0,)), ((), ())), preferred_element_type=jnp.float32
    )


def plain_times(left_matrix, right_matrix):
    return jnp.dot(left_matrix, right_matrix, preferred_element_type=jnp.float32)


def rms_scale(tensor_in):
    return lax.rsqrt(jnp.mean(tensor_in * tensor_in, axis=-1, keepdims=True) + NORM_EPS)


def norm_backward(grad_in, normed, norm_scale, gain_row):
    scaled = grad_in * (1.0 + gain_row)
    return norm_scale * (scaled - normed * jnp.mean(scaled * normed, axis=-1, keepdims=True))


def rope_tables(positions):
    half_width = HEAD_SIZE // 2
    frequency = ROPE_THETA ** (-2.0 * jnp.arange(half_width, dtype=jnp.float32) / HEAD_SIZE)
    angles = positions.astype(jnp.float32)[:, None] * frequency[None, :]
    return (jnp.cos(angles), jnp.sin(angles))


def rotary_heads(tensor_in, cosine_lookup, sine_lookup, direction):
    half_width = HEAD_SIZE // 2
    first_half = tensor_in[..., :half_width]
    second_half = tensor_in[..., half_width:]
    cos_rows = cosine_lookup[:, None, :]
    sin_rows = sine_lookup[:, None, :] * direction
    return jnp.concatenate(
        [
            first_half * cos_rows - second_half * sin_rows,
            second_half * cos_rows + first_half * sin_rows,
        ],
        axis=-1,
    )


def split_weights(attn_full, ffn_full):
    query_width = QUERY_HEADS * HEAD_SIZE
    key_value_width = KEY_VALUE_HEADS * HEAD_SIZE
    return (
        attn_full[:query_width],
        attn_full[query_width : query_width + key_value_width],
        attn_full[query_width + key_value_width : query_width + 2 * key_value_width],
        attn_full[query_width + 2 * key_value_width :],
        ffn_full[:FF],
        ffn_full[FF : 2 * FF],
        ffn_full[2 * FF :],
    )


def adamw_update(parameter, gradient, moments, decay_rate):
    first_moment = BETA_ONE * moments[0] + (1.0 - BETA_ONE) * gradient
    second_moment = BETA_TWO * moments[1] + (1.0 - BETA_TWO) * gradient * gradient
    first_hat = first_moment / (1.0 - BETA_ONE**STEP)
    second_hat = second_moment / (1.0 - BETA_TWO**STEP)
    updated = parameter - LEARN_RATE * (
        first_hat / (jnp.sqrt(second_hat) + ADAM_EPS) + decay_rate * parameter
    )
    return (updated, jnp.stack([first_moment, second_moment]))


def on_device(
    block_input,
    cotangent,
    documents,
    attn_weights,
    ffn_weights,
    norm_gains,
    attn_moments,
    ffn_moments,
    gain_moments,
):
    local_rows = block_input.shape[1]
    heads_per_group = QUERY_HEADS // KEY_VALUE_HEADS
    query_width = QUERY_HEADS * HEAD_SIZE
    key_value_width = KEY_VALUE_HEADS * HEAD_SIZE
    score_scale = HEAD_SIZE ** (-0.5)
    grad_factor = float(local_rows * lax.axis_size(("fsdp", "context"))) ** (-0.5)
    attn_full, ffn_full = (
        lax.all_gather(attn_weights.astype(jnp.bfloat16), ("fsdp", "context"), axis=0, tiled=True),
        lax.all_gather(ffn_weights.astype(jnp.bfloat16), ("fsdp", "context"), axis=0, tiled=True),
    )
    w_query, key_weight, value_weight, w_out, w_gate, w_up, w_down = split_weights(
        attn_full, ffn_full
    )
    own_docs = documents[0]
    all_docs = lax.all_gather(own_docs, "context", axis=0, tiled=True)
    query_index = lax.axis_index("context") * local_rows + jnp.arange(local_rows, dtype=jnp.int32)
    doc_starts = jnp.sum((all_docs[None, :] < own_docs[:, None]).astype(jnp.int32), axis=1)
    cosine_lookup, sine_lookup = rope_tables(query_index - doc_starts)

    def block_mask(key_first, key_width):
        key_index = key_first + jnp.arange(key_width, dtype=jnp.int32)
        key_docs = lax.dynamic_slice_in_dim(all_docs, key_first, key_width, 0)
        return (key_index[None, :] <= query_index[:, None]) & (
            key_docs[None, :] == own_docs[:, None]
        )

    residual = block_input[0].astype(jnp.float32)
    scale_one = rms_scale(residual)
    normed_one = residual * scale_one
    first_hidden = (normed_one * (1.0 + norm_gains[0])).astype(jnp.bfloat16)
    query_matrix = rotary_heads(
        product_transposed(first_hidden, w_query).reshape(local_rows, QUERY_HEADS, HEAD_SIZE),
        cosine_lookup,
        sine_lookup,
        1.0,
    ).astype(jnp.bfloat16)
    key_flat = (
        rotary_heads(
            product_transposed(first_hidden, key_weight).reshape(
                local_rows, KEY_VALUE_HEADS, HEAD_SIZE
            ),
            cosine_lookup,
            sine_lookup,
            1.0,
        )
        .astype(jnp.bfloat16)
        .reshape(local_rows, key_value_width)
    )
    value_flat = product_transposed(first_hidden, value_weight).astype(jnp.bfloat16)
    grouped_queries = query_matrix.reshape(local_rows, KEY_VALUE_HEADS, heads_per_group, HEAD_SIZE)
    start_pair = (
        jnp.zeros((KEY_VALUE_HEADS, heads_per_group, local_rows, HEAD_SIZE), jnp.float32),
        jnp.zeros((KEY_VALUE_HEADS, heads_per_group, local_rows), jnp.float32),
    )
    key_piece = lax.all_gather(key_flat, "context", axis=0, tiled=True)
    value_piece = lax.all_gather(value_flat, "context", axis=0, tiled=True)
    piece_rows = key_piece.shape[0]
    inner_rows = math.gcd(piece_rows, 512)

    def sub_block(sub_index, inner_pair):
        out_sum, total_sum = inner_pair
        offset = sub_index * inner_rows
        key_block = lax.dynamic_slice_in_dim(key_piece, offset, inner_rows, 0).reshape(
            inner_rows, KEY_VALUE_HEADS, HEAD_SIZE
        )
        value_block = lax.dynamic_slice_in_dim(value_piece, offset, inner_rows, 0).reshape(
            inner_rows, KEY_VALUE_HEADS, HEAD_SIZE
        )
        allowed = block_mask(offset, inner_rows)
        scores = (
            jnp.einsum(
                "qhgd,khd->hgqk", grouped_queries, key_block, preferred_element_type=jnp.float32
            )
            * score_scale
        )
        exponent = jnp.where(allowed[None, None], jnp.exp(scores), 0.0)
        out_sum = out_sum + jnp.einsum(
            "hgqk,khd->hgqd",
            exponent.astype(jnp.bfloat16),
            value_block,
            preferred_element_type=jnp.float32,
        )
        return (out_sum, total_sum + jnp.sum(exponent, axis=-1))

    out_sum, totals = lax.fori_loop(0, piece_rows // inner_rows, sub_block, start_pair)
    log_totals = jnp.log(totals)
    attended_rows = (
        (out_sum / totals[..., None])
        .transpose(2, 0, 1, 3)
        .reshape(local_rows, query_width)
        .astype(jnp.bfloat16)
    )
    middle = residual + plain_times(attended_rows, w_out)
    scale_two = rms_scale(middle)
    normed_two = middle * scale_two
    hidden_two = (normed_two * (1.0 + norm_gains[1])).astype(jnp.bfloat16)
    gate_pre = product_transposed(hidden_two, w_gate)
    up_pre = product_transposed(hidden_two, w_up)
    sigmoid_gate = jax.nn.sigmoid(gate_pre)
    activated = (gate_pre * sigmoid_gate * up_pre).astype(jnp.bfloat16)
    block_out = middle + plain_times(activated, w_down)
    attn_back, ffn_back = (
        lax.all_gather(attn_weights.astype(jnp.bfloat16), ("fsdp", "context"), axis=0, tiled=True),
        lax.all_gather(ffn_weights.astype(jnp.bfloat16), ("fsdp", "context"), axis=0, tiled=True),
    )
    w_query, key_weight, value_weight, w_out, w_gate, w_up, w_down = split_weights(
        attn_back, ffn_back
    )
    seq_cotangent = cotangent[0]
    grad_act = product_transposed(seq_cotangent, w_down)
    grad_gate = (grad_act * up_pre * sigmoid_gate * (1.0 + gate_pre * (1.0 - sigmoid_gate))).astype(
        jnp.bfloat16
    )
    grad_up = (grad_act * gate_pre * sigmoid_gate).astype(jnp.bfloat16)
    ffn_term = (
        jnp.concatenate(
            [
                transposed_times(grad_gate, hidden_two),
                transposed_times(grad_up, hidden_two),
                transposed_times(activated, seq_cotangent),
            ],
            axis=0,
        )
        * grad_factor
    )
    grad_hidden_two = plain_times(grad_gate, w_gate) + plain_times(grad_up, w_up)
    gain_two = jnp.sum(grad_hidden_two * normed_two, axis=0)
    grad_middle = seq_cotangent.astype(jnp.float32) + norm_backward(
        grad_hidden_two, normed_two, scale_two, norm_gains[1]
    )
    grad_middle_bf = grad_middle.astype(jnp.bfloat16)
    grad_w_out = transposed_times(attended_rows, grad_middle_bf)
    attended_gradient = product_transposed(grad_middle_bf, w_out).astype(jnp.bfloat16)
    group_gradient = attended_gradient.reshape(
        local_rows, KEY_VALUE_HEADS, heads_per_group, HEAD_SIZE
    )
    row_delta = jnp.sum(
        group_gradient.astype(jnp.float32)
        * attended_rows.reshape(local_rows, KEY_VALUE_HEADS, heads_per_group, HEAD_SIZE).astype(
            jnp.float32
        ),
        axis=-1,
    ).transpose(1, 2, 0)
    seq_rows = local_rows * lax.axis_size("context")
    start_three = (
        jnp.zeros((KEY_VALUE_HEADS, heads_per_group, local_rows, HEAD_SIZE), jnp.float32),
        jnp.zeros((seq_rows, key_value_width), jnp.float32),
        jnp.zeros((seq_rows, key_value_width), jnp.float32),
    )
    attend_key_piece = lax.all_gather(key_flat, "context", axis=0, tiled=True)
    attend_value_piece = lax.all_gather(value_flat, "context", axis=0, tiled=True)
    piece_rows = attend_key_piece.shape[0]
    attend_inner_rows = math.gcd(piece_rows, 512)

    def sub_block(sub_index, inner_three):
        grad_query, grad_key_all, grad_value_all = inner_three
        offset = sub_index * attend_inner_rows
        key_block = lax.dynamic_slice_in_dim(
            attend_key_piece, offset, attend_inner_rows, 0
        ).reshape(attend_inner_rows, KEY_VALUE_HEADS, HEAD_SIZE)
        value_block = lax.dynamic_slice_in_dim(
            attend_value_piece, offset, attend_inner_rows, 0
        ).reshape(attend_inner_rows, KEY_VALUE_HEADS, HEAD_SIZE)
        allowed = block_mask(offset, attend_inner_rows)
        scores = (
            jnp.einsum(
                "qhgd,khd->hgqk", grouped_queries, key_block, preferred_element_type=jnp.float32
            )
            * score_scale
        )
        probabilities = jnp.where(allowed[None, None], jnp.exp(scores - log_totals[..., None]), 0.0)
        grad_probs = jnp.einsum(
            "qhgd,khd->hgqk", group_gradient, value_block, preferred_element_type=jnp.float32
        )
        grad_scores = (probabilities * (grad_probs - row_delta[..., None]) * score_scale).astype(
            jnp.bfloat16
        )
        grad_query = grad_query + jnp.einsum(
            "hgqk,khd->hgqd", grad_scores, key_block, preferred_element_type=jnp.float32
        )
        key_part = jnp.einsum(
            "hgqk,qhgd->khd", grad_scores, grouped_queries, preferred_element_type=jnp.float32
        ).reshape(attend_inner_rows, key_value_width)
        value_part = jnp.einsum(
            "hgqk,qhgd->khd",
            probabilities.astype(jnp.bfloat16),
            group_gradient,
            preferred_element_type=jnp.float32,
        ).reshape(attend_inner_rows, key_value_width)
        grad_key_all = lax.dynamic_update_slice_in_dim(grad_key_all, key_part, offset, 0)
        grad_value_all = lax.dynamic_update_slice_in_dim(grad_value_all, value_part, offset, 0)
        return (grad_query, grad_key_all, grad_value_all)

    grad_query_sum, grad_key_all, grad_value_all = lax.fori_loop(
        0, piece_rows // attend_inner_rows, sub_block, start_three
    )
    key_gradient_rows, grad_values = (
        lax.psum_scatter(
            grad_key_all.astype(jnp.bfloat16), "context", scatter_dimension=0, tiled=True
        ).astype(jnp.float32),
        lax.psum_scatter(
            grad_value_all.astype(jnp.bfloat16), "context", scatter_dimension=0, tiled=True
        ).astype(jnp.float32),
    )
    grad_q_bf = (
        rotary_heads(
            grad_query_sum.transpose(2, 0, 1, 3).reshape(local_rows, QUERY_HEADS, HEAD_SIZE),
            cosine_lookup,
            sine_lookup,
            -1.0,
        )
        .reshape(local_rows, query_width)
        .astype(jnp.bfloat16)
    )
    grad_k_bf = (
        rotary_heads(
            key_gradient_rows.reshape(local_rows, KEY_VALUE_HEADS, HEAD_SIZE),
            cosine_lookup,
            sine_lookup,
            -1.0,
        )
        .reshape(local_rows, key_value_width)
        .astype(jnp.bfloat16)
    )
    grad_v_bf = grad_values.astype(jnp.bfloat16)
    attn_term = (
        jnp.concatenate(
            [
                transposed_times(grad_q_bf, first_hidden),
                transposed_times(grad_k_bf, first_hidden),
                transposed_times(grad_v_bf, first_hidden),
                grad_w_out,
            ],
            axis=0,
        )
        * grad_factor
    )
    grad_hidden_one = (
        plain_times(grad_q_bf, w_query)
        + plain_times(grad_k_bf, key_weight)
        + plain_times(grad_v_bf, value_weight)
    )
    gain_one = jnp.sum(grad_hidden_one * normed_one, axis=0)
    grad_input = grad_middle + norm_backward(grad_hidden_one, normed_one, scale_one, norm_gains[0])
    gain_term = jnp.stack([gain_one, gain_two]) * grad_factor
    attn_shard, ffn_shard, gain_shard = (
        lax.psum_scatter(attn_term, ("fsdp", "context"), scatter_dimension=0, tiled=True),
        lax.psum_scatter(ffn_term, ("fsdp", "context"), scatter_dimension=0, tiled=True),
        lax.psum_scatter(gain_term, ("fsdp", "context"), scatter_dimension=1, tiled=True),
    )
    column_count = norm_gains.shape[1] // lax.axis_size(("fsdp", "context"))
    own_gains = lax.dynamic_slice_in_dim(
        norm_gains, lax.axis_index(("fsdp", "context")) * column_count, column_count, 1
    )
    new_attn, attn_states = adamw_update(attn_weights, attn_shard, attn_moments, WEIGHT_DECAY)
    new_ffn, ffn_states = adamw_update(ffn_weights, ffn_shard, ffn_moments, WEIGHT_DECAY)
    new_gains, gain_states = adamw_update(own_gains, gain_shard, gain_moments, 0.0)
    return (
        block_out[None],
        grad_input[None],
        attn_shard,
        ffn_shard,
        gain_shard,
        new_attn,
        new_ffn,
        new_gains,
        attn_states,
        ffn_states,
        gain_states,
    )


def solution(mesh):
    placed = (
        P("fsdp", "context", None),
        P("fsdp", "context", None),
        P("fsdp", "context"),
        P(("fsdp", "context"), None),
        P(("fsdp", "context"), None),
        P(),
        P(None, ("fsdp", "context"), None),
        P(None, ("fsdp", "context"), None),
        P(None, None, ("fsdp", "context")),
    )
    return jax.shard_map(
        on_device,
        mesh=mesh,
        in_specs=placed,
        out_specs=(
            P("fsdp", "context", None),
            P("fsdp", "context", None),
            P(("fsdp", "context"), None),
            P(("fsdp", "context"), None),
            P(None, ("fsdp", "context")),
            P(("fsdp", "context"), None),
            P(("fsdp", "context"), None),
            P(None, ("fsdp", "context")),
            P(None, ("fsdp", "context"), None),
            P(None, ("fsdp", "context"), None),
            P(None, None, ("fsdp", "context")),
        ),
        check_vma=False,
    )
```

profile of v0, /device:TPU:0, one launch (start us, length us, event | category | flops | bytes accessed | tf_op | source)
XLA Modules:
  0.0 1589.9 jit_solution(6565524639662273563)
XLA Ops:
  11.3 105.4 %all-gather.6.cloned.1.call-done = bf16[4608,1536]{1,0:T(8,128)(2,1)} async-done(((bf16[144,1536]{1,0:T(8,128)(2,1)}), bf16[4608,1536]{1,0:T(8,128)(2,1)}) %all-gather.6.cloned.1.call-update) | async-done | bytes 14155792 | tf_op jit(solution)/shard_map/all_gather | solution.py:111
  116.7 3.5 fusion.65
  120.3 8.7 all-gather
  138.1 6.3 all-gather.10.cloned.1.call-done
  147.0 25.7 %all-gather.8.cloned.1.call-done = bf16[1024,768]{0,1:T(8,128)(2,1)} async-done(((bf16[128,768]{0,1:T(8,128)(2,1)}), bf16[1024,768]{0,1:T(8,128)(2,1)}) %all-gather.8.cloned.1.call-update) | async-done | bytes 1572880 | tf_op jit(solution)/shard_map/all_gather | solution.py:158
  172.7 16.3 %while.34 = (s32[]{:T(128)}, f32[8,2,128,96]{2,3,1,0:T(8,128)S(1)}, f32[8,2,128]{2,1,0:T(2,128)S(1)}, s32[1024]{0:T(1024)S(1)}, s32[1,128]{1,0:T(1,128)S(1)}, /*...) while((s32[]{:T(128)}, f32[8,2,128,96]{2,3,1,0:T(8,128)S(1)}, ...), condition=%wide.region_4.5_spmd.clone, body=%wide.region_2.4_spmd.clone.sunk | while | flops 409537152 | bytes 15314638 | solution.py:188
  177.5 3.1 fusion.177
  185.5 3.4 fusion.177
  189.1 3.4 multiply_reduce_fusion.3
  192.6 197.7 %all-gather.12.cloned.1.call-done = bf16[12288,1536]{1,0:T(8,128)(2,1)} async-done(((bf16[384,1536]{1,0:T(8,128)(2,1)}), bf16[12288,1536]{1,0:T(8,128)(2,1)}) %all-gather.12.cloned.1.call-update) | async-done | bytes 37748752 | tf_op jit(solution)/shard_map/all_gather | solution.py:112
  390.4 7.0 fusion.30
  397.4 7.1 fusion.36
  404.5 8.4 multiply_convert_fusion.1
  412.9 6.4 fusion.34
  419.4 6.1 multiply_reduce_fusion
  433.4 28.3 %while.35 = (s32[]{:T(128)}, f32[8,2,128,96]{2,3,1,0:T(8,128)}, bf16[1024,768]{0,1:T(8,128)(2,1)}, bf16[1024,768]{0,1:T(8,128)(2,1)}, s32[1024]{0:T(1024)S(1)}, ...) while((s32[]{:T(128)}, f32[8,2,128,96]{2,3,1,0:T(8,128)}, ...), condition=%wide.region_9.10_spmd.clone, body=%wide.region_8.9_spmd.clone.sunk | while | flops 1018757760 | bytes 91197336 | solution.py:297
  466.3 3.3 fusion.114
  469.6 5.0 fusion.96
  474.6 4.9 fusion.99
  479.6 21.5 %reduce-scatter.16.cloned.1.call-done = bf16[128,768]{1,0:T(8,128)(2,1)} async-done(((bf16[1024,768]{1,0:T(8,128)(2,1)}), bf16[128,768]{1,0:T(8,128)(2,1)}) %reduce-scatter.16.cloned.1.call-update) | async-done | bytes 196624
  507.5 35.7 %reduce-scatter.18.cloned.1.call-done = bf16[128,768]{1,0:T(8,128)(2,1)} async-done(((bf16[1024,768]{1,0:T(8,128)(2,1)}), bf16[128,768]{1,0:T(8,128)(2,1)}) %reduce-scatter.18.cloned.1.call-update) | async-done | bytes 196624
  543.2 3.2 fusion.81
  550.1 18.1 %maximum_multiply_fusion.1 = f32[4608,1536]{1,0:T(8,128)} fusion(f32[1536,1536]{1,0:T(8,128)} %fusion.99, f32[768,1536]{1,0:T(8,128)S(1)} %fusion.103, f32[768,1536]{1,0:T(8,128)S(1)} %copy-done.5, f32[1536,1536]{1,0:T(8,128)} %fusion.96), kind=kLoop, calls=%fused_computation.42 | loop fusion | flops 28311552 | bytes 56623104 | tf_op jit(solution)/shard_map/mul | solution.py:330
  569.1 11.5 fusion.119
  580.7 10.2 fusion.118
  590.9 10.2 fusion.87
  601.0 51.5 %maximum_multiply_fusion = f32[12288,1536]{1,0:T(8,128)} fusion(f32[4096,1536]{1,0:T(8,128)} %fusion.87, f32[4096,1536]{1,0:T(8,128)} %fusion.119, f32[4096,1536]{1,0:T(8,128)} %fusion.118), kind=kLoop, calls=%fused_computation.41 | loop fusion | flops 56623104 | bytes 150994944 | tf_op jit(solution)/shard_map/mul | solution.py:219
  653.7 8.5 fusion.55
  666.1 248.1 %reduce-scatter.12.cloned.1.call-done = f32[144,1536]{1,0:T(8,128)} async-done(((f32[4608,1536]{1,0:T(8,128)}), f32[144,1536]{1,0:T(8,128)}) %reduce-scatter.12.cloned.1.call-update) | async-done | bytes 884752 | tf_op jit(solution)/shard_map/reduce_scatter | solution.py:350
  914.2 3.3 fusion.98
  918.8 655.4 %reduce-scatter.14.cloned.1.call-done = f32[384,1536]{1,0:T(8,128)} async-done(((f32[12288,1536]{1,0:T(8,128)}), f32[384,1536]{1,0:T(8,128)}) %reduce-scatter.14.cloned.1.call-update) | async-done | bytes 2359312 | tf_op jit(solution)/shard_map/reduce_scatter | solution.py:351
  1574.2 6.3 fusion.85
  (198 shorter events, 85.6 us)
Async XLA Ops:
  7.2 113.1 %copy-start.29 = (s32[1,128]{1,0:T(1,128)S(1)}, s32[1,128]{1,0:T(1,128)}, u32[]{:S(2)}) copy-start(s32[1,128]{1,0:T(1,128)} %param.15) | copy-start | bytes 1540
  7.2 109.5 %all-gather.6.cloned.1.call-start = ((), (), s32[]{:S(2)}) async-start(), calls=%async_computation.5 | async-start | bytes 14598144 | tf_op jit(solution)/shard_map/all_gather | solution.py:111
  9.2 135.2 %all-gather.10.cloned.1.call-start = ((), (), s32[]{:S(2)}) async-start(), calls=%async_computation.7 | async-start | bytes 1769472 | tf_op jit(solution)/shard_map/all_gather | solution.py:159
  116.7 12.8 slice-start.4
  116.7 12.8 copy-start.3
  120.3 52.4 %all-gather.8.cloned.1.call-start = ((), (), s32[]{:S(2)}) async-start(), calls=%async_computation.6 | async-start | bytes 1769472 | tf_op jit(solution)/shard_map/all_gather | solution.py:158
  131.1 259.3 %all-gather.12.cloned.1.call-start = ((), (), s32[]{:S(2)}) async-start(), calls=%async_computation.8 | async-start | bytes 38928384 | tf_op jit(solution)/shard_map/all_gather | solution.py:112
  134.0 367.1 %reduce-scatter.16.cloned.1.call-start = ((), (), s32[]{:S(2)}) async-start(), calls=%async_computation.11 | async-start | bytes 1769472
  189.0 201.4 %copy-start.21 = (bf16[1,128,1536]{2,1,0:T(8,128)(2,1)S(1)}, bf16[1,128,1536]{2,1,0:T(8,128)(2,1)}, u32[]{:S(2)}) copy-start(bf16[1,128,1536]{2,1,0:T(8,128)(2,1)} %param.14) | copy-start | bytes 1179652
  192.5 226.9 %copy-start.17 = (f32[128,1536]{1,0:T(8,128)}, f32[128,1536]{1,0:T(8,128)S(1)}, u32[]{:S(2)}) copy-start(f32[128,1536]{1,0:T(8,128)S(1)} %get-tuple-element.633) | copy-start | bytes 2359300
  192.6 211.9 %copy-start.15 = (bf16[128,1536]{1,0:T(8,128)(2,1)}, bf16[128,1536]{1,0:T(8,128)(2,1)S(1)}, u32[]{:S(2)}) copy-start(bf16[128,1536]{1,0:T(8,128)(2,1)S(1)} %multiply_convert_fusion.3) | copy-start | bytes 1179652
  412.9 6.4 copy-start.26
  412.9 6.5 copy-start.24
  412.9 14.0 slice-start
  412.9 14.0 slice-start.1
  419.4 7.6 slice-start.2
  419.4 7.6 slice-start.3
  449.5 4.7 copy-start
  464.4 78.8 %reduce-scatter.18.cloned.1.call-start = ((), (), s32[]{:S(2)}) async-start(), calls=%async_computation.12 | async-start | bytes 1769472
  466.2 197.1 %reduce-scatter.20.cloned.1.call-start = ((), (), s32[]{:S(2)}) async-start(), calls=%async_computation.13 | async-start | bytes 811008
  469.6 5.1 copy-start.8
  469.6 5.1 copy-start.20
  547.7 366.5 %reduce-scatter.12.cloned.1.call-start = ((), (), s32[]{:S(2)}) async-start(), calls=%async_computation.9 | async-start | bytes 29196288 | tf_op jit(solution)/shard_map/reduce_scatter | solution.py:350
  568.1 12.5 copy-start.25
  568.1 1006.1 %reduce-scatter.14.cloned.1.call-start = ((), (), s32[]{:S(2)}) async-start(), calls=%async_computation.10 | async-start | bytes 77856768 | tf_op jit(solution)/shard_map/reduce_scatter | solution.py:351
  580.7 10.2 copy-start.22
  580.7 10.2 copy-start.23
  653.7 8.5 copy-start.27
  653.7 10.5 copy-start.31
  653.7 260.5 %copy-start.14 = (f32[144,1536]{1,0:T(8,128)S(1)}, f32[144,1536]{1,0:T(8,128)}, u32[]{:S(2)}) copy-start(f32[144,1536]{1,0:T(8,128)} %param.16) | copy-start | bytes 2654212
  664.2 254.6 %copy-start.30 = (f32[2,48]{1,0:T(2,128)}, f32[2,48]{1,0:T(2,128)S(1)}, u32[]{:S(2)}) copy-start(f32[2,48]{1,0:T(2,128)S(1)} %copy.64) | copy-start | bytes 1156
  666.1 908.1 %copy-start.6 = (f32[384,1536]{1,0:T(8,128)S(1)}, f32[384,1536]{1,0:T(8,128)}, u32[]{:S(2)}) copy-start(f32[384,1536]{1,0:T(8,128)} %param.17) | copy-start | bytes 7077892
  (21 other events, 55.9 us)
Sparse Core Ops, SparseCore 0:
  11.5 105.2 all-gather.5
  120.4 23.9 all-gather.9
  146.9 25.7 all-gather.7
  176.0 214.3 all-gather.11
  464.5 36.5 reduce-scatter.15
  504.8 38.3 reduce-scatter.17
  548.9 96.1 reduce-scatter.19
  652.1 262.0 reduce-scatter.11
  921.2 653.0 reduce-scatter.13
where the time goes:
time: 1600 us; the launch traced here: 1590 us
  waiting for transfers between devices  1300 us (81%)
  matrix products  138 us (9%)
  other arithmetic  98 us (6%)
  local copies, waits for them, and re-layouts  33.7 us (2%)
    reduce_scatter x1, waiting for transfers between devices, on_device(): lax.psum_scatter(ffn_term, ('fsdp', 'context'), scatter_dimension=0, tile...  655 us
    reduce_scatter x1, waiting for transfers between devices, on_device(): lax.psum_scatter(attn_term, ('fsdp', 'context'), scatter_dimension=0, til...  248 us
    all_gather x1, waiting for transfers between devices, on_device(): lax.all_gather(ffn_weights.astype(jnp.bfloat16), ('fsdp', 'context'), axi...  198 us
    all_gather x1, waiting for transfers between devices, on_device(): lax.all_gather(attn_weights.astype(jnp.bfloat16), ('fsdp', 'context'), ax...  105 us
    unnamed x12, waiting for transfers between devices  57.3 us
    mul x1, other arithmetic, on_device(): jnp.concatenate([transposed_times(grad_gate, hidden_two), transposed_time...  51.5 us
    dot_general x7, matrix products, transposed_times(): lax.dot_general(left_matrix, right_matrix, (((0,), (0,)), ((), ())), pref...  45.8 us
    dot_general x7, matrix products, plain_times(): jnp.dot(left_matrix, right_matrix, preferred_element_type=jnp.float32)  33 us
  transfers between devices with their start and end apart: 9, of which 8 were waited for; matrix products, arithmetic and copies ran while one was open for 11% of the time, Pallas kernels for 0%

commit v1 on v0

--- a/solution.py
+++ b/solution.py
@@ -16,6 +16,18 @@
 ADAM_EPS = 1e-08
 LEARN_RATE = 0.02
 WEIGHT_DECAY = 0.1
+
+
+def gather_by_bits(x, axis, dim):
+    ways, here = (lax.axis_size(axis), lax.axis_index(axis))
+    grown, reach = (x, 1)
+    while reach < ways:
+        theirs = lax.ppermute(grown, axis, [(d, d ^ reach) for d in range(ways)])
+        mine_first = jnp.concatenate([grown, theirs], axis=dim)
+        theirs_first = jnp.concatenate([theirs, grown], axis=dim)
+        grown = jnp.where(here & reach == 0, mine_first, theirs_first)
+        reach = 2 * reach
+    return grown
 
 
 def product_transposed(left_matrix, right_matrix):
@@ -108,7 +120,7 @@
     score_scale = HEAD_SIZE ** (-0.5)
     grad_factor = float(local_rows * lax.axis_size(("fsdp", "context"))) ** (-0.5)
     attn_full, ffn_full = (
-        lax.all_gather(attn_weights.astype(jnp.bfloat16), ("fsdp", "context"), axis=0, tiled=True),
+        gather_by_bits(attn_weights.astype(jnp.bfloat16), ("fsdp", "context"), 0),
         lax.all_gather(ffn_weights.astype(jnp.bfloat16), ("fsdp", "context"), axis=0, tiled=True),
     )
     w_query, key_weight, value_weight, w_out, w_gate, w_up, w_down = split_weights(

time: 1600 us -> 2040 us (1.27)
  waiting for transfers between devices: 1300 us -> 1700 us
  other arithmetic: 98 us -> 120 us
    ppermute x0 -> x5, waiting for transfers between devices: none -> 438 us  [gather_by_bits(): theirs = lax.ppermute(grown, axis, [(d, d ^ reach) for d in range(ways)])]
    all_gather x1, waiting for transfers between devices: 105 us -> 68.4 us  [on_device(): lax.all_gather(attn_weights.astype(jnp.bfloat16), ('fsdp', 'context'), ax...]
    select_n x0 -> x5, other arithmetic: none -> 26.1 us  [gather_by_bits(): grown = jnp.where(here & reach == 0, mine_first, theirs_first)]
  transfers between devices with their start and end apart: 9 -> 14, of which waited for: 8 -> 13; matrix products, arithmetic and copies ran while one was open for 11% -> 10% of each run, Pallas kernels for 0% -> 0%
where the time goes in v1:
time: 2040 us; the launch traced here: 2030 us
  waiting for transfers between devices  1700 us (83%)
  matrix products  138 us (7%)
  other arithmetic  120 us (6%)
  local copies, waits for them, and re-layouts  38.7 us (2%)
    reduce_scatter x1, waiting for transfers between devices, on_device(): lax.psum_scatter(ffn_term, ('fsdp', 'context'), scatter_dimension=0, tile...  656 us
    ppermute x5, waiting for transfers between devices, gather_by_bits(): theirs = lax.ppermute(grown, axis, [(d, d ^ reach) for d in range(ways)])  438 us
    reduce_scatter x1, waiting for transfers between devices, on_device(): lax.psum_scatter(attn_term, ('fsdp', 'context'), scatter_dimension=0, til...  248 us
    all_gather x1, waiting for transfers between devices, on_device(): lax.all_gather(ffn_weights.astype(jnp.bfloat16), ('fsdp', 'context'), axi...  198 us
    all_gather x1, waiting for transfers between devices, on_device(): lax.all_gather(attn_weights.astype(jnp.bfloat16), ('fsdp', 'context'), ax...  68.4 us
    unnamed x12, waiting for transfers between devices  58.1 us
    mul x1, other arithmetic, on_device(): jnp.concatenate([transposed_times(grad_gate, hidden_two), transposed_time...  51.4 us
    dot_general x7, matrix products, transposed_times(): lax.dot_general(left_matrix, right_matrix, (((0,), (0,)), ((), ())), pref...  45.8 us
  transfers between devices with their start and end apart: 14, of which 13 were waited for; matrix products, arithmetic and copies ran while one was open for 10% of the time, Pallas kernels for 0%

profile of v1, /device:TPU:0, one launch (start us, length us, event | category | flops | bytes accessed | tf_op | source)
XLA Modules:
  0.0 2030.8 jit_solution(17074950280520263205)
XLA Ops:
  13.6 20.1 collective-permute-done.1
  37.5 38.4 %collective-permute-done.2 = bf16[576,1536]{1,0:T(8,128)(2,1)} collective-permute-done((bf16[576,1536]{1,0:T(8,128)(2,1)S(1)}, bf16[576,1536]{1,0:T(8,128)(2,1)}, u32[]{:S(2)}, u32[]{:S(2)}) %collective-permute-start.2) | collective-permute-done | bytes 1769504 | tf_op jit(solution)/shard_map/ppermute | solution.py:25
  81.2 75.9 %collective-permute-done.3 = bf16[1152,1536]{1,0:T(8,128)(2,1)} collective-permute-done((bf16[1152,1536]{1,0:T(8,128)(2,1)}, bf16[1152,1536]{1,0:T(8,128)(2,1)}, u32[]{:S(2)}, u32[]{:S(2)}) %collective-permute-start.3) | collective-permute-done | bytes 3538976 | tf_op jit(solution)/shard_map/ppermute | solution.py:25
  157.1 8.7 maximum_select_fusion.1
  168.3 302.5 %collective-permute-done.4 = bf16[2304,1536]{1,0:T(8,128)(2,1)} collective-permute-done((bf16[2304,1536]{1,0:T(8,128)(2,1)}, bf16[2304,1536]{1,0:T(8,128)(2,1)}, u32[]{:S(2)}, u32[]{:S(2)}) %collective-permute-start.4) | collective-permute-done | bytes 7077920 | tf_op jit(solution)/shard_map/ppermute | solution.py:25
  470.9 11.3 maximum_select_fusion
  482.2 5.0 copy-done.2
  488.9 8.3 all-gather
  507.3 7.8 all-gather.8.cloned.1.call-done
  517.7 25.7 %all-gather.6.cloned.1.call-done = bf16[1024,768]{0,1:T(8,128)(2,1)} async-done(((bf16[128,768]{0,1:T(8,128)(2,1)}), bf16[1024,768]{0,1:T(8,128)(2,1)}) %all-gather.6.cloned.1.call-update) | async-done | bytes 1572880 | tf_op jit(solution)/shard_map/all_gather | solution.py:170
  543.4 16.3 while.34
  563.4 197.9 %all-gather.10.cloned.1.call-done = bf16[12288,1536]{1,0:T(8,128)(2,1)} async-done(((bf16[384,1536]{1,0:T(8,128)(2,1)}), bf16[12288,1536]{1,0:T(8,128)(2,1)}) %all-gather.10.cloned.1.call-update) | async-done | bytes 37748752 | tf_op jit(solution)/shard_map/all_gather | solution.py:124
  761.3 7.0 fusion.30
  768.3 7.2 fusion.36
  775.5 8.4 multiply_convert_fusion.1
  784.0 6.4 fusion.34
  790.4 6.2 multiply_reduce_fusion
  796.9 68.4 %all-gather.12.cloned.1.call-done = bf16[4608,1536]{1,0:T(8,128)(2,1)} async-done(((bf16[144,1536]{1,0:T(8,128)(2,1)}), bf16[4608,1536]{1,0:T(8,128)(2,1)}) %all-gather.12.cloned.1.call-update) | async-done | bytes 14155792 | tf_op jit(solution)/shard_map/all_gather | solution.py:218
  874.0 28.3 %while.35 = (s32[]{:T(128)}, f32[8,2,128,96]{2,3,1,0:T(8,128)}, bf16[1024,768]{0,1:T(8,128)(2,1)}, bf16[1024,768]{0,1:T(8,128)(2,1)}, s32[1024]{0:T(1024)S(1)}, ...) while((s32[]{:T(128)}, f32[8,2,128,96]{2,3,1,0:T(8,128)}, ...), condition=%wide.region_9.10_spmd.clone, body=%wide.region_8.9_spmd.clone.sunk | while | flops 1018757760 | bytes 91197336 | solution.py:309
  910.2 5.0 fusion.99
  915.2 4.9 fusion.102
  920.1 21.8 %reduce-scatter.16.cloned.1.call-done = bf16[128,768]{1,0:T(8,128)(2,1)} async-done(((bf16[1024,768]{1,0:T(8,128)(2,1)}), bf16[128,768]{1,0:T(8,128)(2,1)}) %reduce-scatter.16.cloned.1.call-update) | async-done | bytes 196624
  948.4 35.6 %reduce-scatter.18.cloned.1.call-done = bf16[128,768]{1,0:T(8,128)(2,1)} async-done(((bf16[1024,768]{1,0:T(8,128)(2,1)}), bf16[128,768]{1,0:T(8,128)(2,1)}) %reduce-scatter.18.cloned.1.call-update) | async-done | bytes 196624
  990.9 17.9 maximum_multiply_fusion.1
  1009.8 11.6 fusion.119
  1021.4 10.2 fusion.118
  1031.6 10.2 fusion.90
  1041.7 51.4 %maximum_multiply_fusion = f32[12288,1536]{1,0:T(8,128)} fusion(f32[4096,1536]{1,0:T(8,128)} %fusion.90, f32[4096,1536]{1,0:T(8,128)} %fusion.119, f32[4096,1536]{1,0:T(8,128)} %fusion.118), kind=kLoop, calls=%fused_computation.41 | loop fusion | flops 56623104 | bytes 150994944 | tf_op jit(solution)/shard_map/mul | solution.py:231
  1094.3 8.3 fusion.57
  1106.5 248.5 %reduce-scatter.12.cloned.1.call-done = f32[144,1536]{1,0:T(8,128)} async-done(((f32[4608,1536]{1,0:T(8,128)}), f32[144,1536]{1,0:T(8,128)}) %reduce-scatter.12.cloned.1.call-update) | async-done | bytes 884752 | tf_op jit(solution)/shard_map/reduce_scatter | solution.py:362
  1359.6 655.6 %reduce-scatter.14.cloned.1.call-done = f32[384,1536]{1,0:T(8,128)} async-done(((f32[12288,1536]{1,0:T(8,128)}), f32[384,1536]{1,0:T(8,128)}) %reduce-scatter.14.cloned.1.call-update) | async-done | bytes 2359312 | tf_op jit(solution)/shard_map/reduce_scatter | solution.py:363
  2015.3 6.3 fusion.88
  (212 shorter events, 123.0 us)
Async XLA Ops:
  7.2 508.0 %all-gather.8.cloned.1.call-start = ((), (), s32[]{:S(2)}) async-start(), calls=%async_computation.6 | async-start | bytes 1769472 | tf_op jit(solution)/shard_map/all_gather | solution.py:171
  8.4 71.2 %copy-start.15 = (bf16[144,1536]{1,0:T(8,128)(2,1)}, bf16[144,1536]{1,0:T(8,128)(2,1)S(1)}, u32[]{:S(2)}) copy-start(bf16[144,1536]{1,0:T(8,128)(2,1)S(1)} %convert_element_type.151) | copy-start | bytes 1327108
  8.5 2.0 collective-permute-start
  10.6 23.0 %collective-permute-start.1 = (bf16[288,1536]{1,0:T(8,128)(2,1)S(1)}, bf16[288,1536]{1,0:T(8,128)(2,1)}, u32[]{:S(2)}, u32[]{:S(2)}) collective-permute-start(bf16[288,1536]{1,0:T(8,128)(2,1)S(1)} %maximum_select_fusion.4), channel_id=1, source_target_pairs={{0,2},{1,3},{2,0},{3,1},{4,6},{5,7},{6,4},{7,5},{8,10},{9,11},{10,... | collective-permute-start | bytes 2654216 | tf_op jit(solution)/shard_map/ppermute | solution.py:25
  35.7 40.2 %collective-permute-start.2 = (bf16[576,1536]{1,0:T(8,128)(2,1)S(1)}, bf16[576,1536]{1,0:T(8,128)(2,1)}, u32[]{:S(2)}, u32[]{:S(2)}) collective-permute-start(bf16[576,1536]{1,0:T(8,128)(2,1)S(1)} %maximum_select_fusion.3), channel_id=1, source_target_pairs={{0,4},{1,5},{2,6},{3,7},{4,0},{5,1},{6,2},{7,3},{8,12},{9,13},{10,... | collective-permute-start | bytes 5308424 | tf_op jit(solution)/shard_map/ppermute | solution.py:25
  79.7 77.5 %collective-permute-start.3 = (bf16[1152,1536]{1,0:T(8,128)(2,1)}, bf16[1152,1536]{1,0:T(8,128)(2,1)}, u32[]{:S(2)}, u32[]{:S(2)}) collective-permute-start(bf16[1152,1536]{1,0:T(8,128)(2,1)} %maximum_select_fusion.2), channel_id=1, source_target_pairs={{0,8},{1,9},{2,10},{3,11},{4,12},{5,13},{6,14},{7,15},{8,0},{9,1},... | collective-permute-start | bytes 10616840 | tf_op jit(solution)/shard_map/ppermute | solution.py:25
  81.2 86.9 %copy-start.33 = (f32[2,1536]{1,0:T(2,128)S(1)}, f32[2,1536]{1,0:T(2,128)}, u32[]{:S(2)}) copy-start(f32[2,1536]{1,0:T(2,128)} %param.18) | copy-start | bytes 36868
  81.2 86.9 %copy-start.4 = (bf16[1,128,1536]{2,1,0:T(8,128)(2,1)S(1)}, bf16[1,128,1536]{2,1,0:T(8,128)(2,1)}, u32[]{:S(2)}) copy-start(bf16[1,128,1536]{2,1,0:T(8,128)(2,1)} %param.13) | copy-start | bytes 1179652
  165.8 305.0 %collective-permute-start.4 = (bf16[2304,1536]{1,0:T(8,128)(2,1)}, bf16[2304,1536]{1,0:T(8,128)(2,1)}, u32[]{:S(2)}, u32[]{:S(2)}) collective-permute-start(bf16[2304,1536]{1,0:T(8,128)(2,1)} %maximum_select_fusion.1), channel_id=1, source_target_pairs={{0,16},{1,17},{2,18},{3,19},{4,20},{5,21},{6,22},{7,23},{8,24},{9,... | collective-permute-start | bytes 21233672 | tf_op jit(solution)/shard_map/ppermute | solution.py:25
  168.3 320.6 %copy-start.32 = (s32[1,128]{1,0:T(1,128)S(1)}, s32[1,128]{1,0:T(1,128)}, u32[]{:S(2)}) copy-start(s32[1,128]{1,0:T(1,128)} %param.15) | copy-start | bytes 1540
  488.8 8.8 slice-start
  488.9 54.5 %all-gather.6.cloned.1.call-start = ((), (), s32[]{:S(2)}) async-start(), calls=%async_computation.5 | async-start | bytes 1769472 | tf_op jit(solution)/shard_map/all_gather | solution.py:170
  499.3 261.9 %all-gather.10.cloned.1.call-start = ((), (), s32[]{:S(2)}) async-start(), calls=%async_computation.7 | async-start | bytes 38928384 | tf_op jit(solution)/shard_map/all_gather | solution.py:124
  502.2 363.1 %all-gather.12.cloned.1.call-start = ((), (), s32[]{:S(2)}) async-start(), calls=%async_computation.8 | async-start | bytes 14598144 | tf_op jit(solution)/shard_map/all_gather | solution.py:218
  502.8 439.2 %reduce-scatter.16.cloned.1.call-start = ((), (), s32[]{:S(2)}) async-start(), calls=%async_computation.11 | async-start | bytes 1769472
  559.7 201.5 %copy-start.23 = (bf16[1,128,1536]{2,1,0:T(8,128)(2,1)S(1)}, bf16[1,128,1536]{2,1,0:T(8,128)(2,1)}, u32[]{:S(2)}) copy-start(bf16[1,128,1536]{2,1,0:T(8,128)(2,1)} %param.14) | copy-start | bytes 1179652
  563.2 233.4 %copy-start.19 = (f32[128,1536]{1,0:T(8,128)}, f32[128,1536]{1,0:T(8,128)S(1)}, u32[]{:S(2)}) copy-start(f32[128,1536]{1,0:T(8,128)S(1)} %get-tuple-element.633) | copy-start | bytes 2359300
  563.4 212.1 %copy-start.17 = (bf16[128,1536]{1,0:T(8,128)(2,1)}, bf16[128,1536]{1,0:T(8,128)(2,1)S(1)}, u32[]{:S(2)}) copy-start(bf16[128,1536]{1,0:T(8,128)(2,1)S(1)} %multiply_convert_fusion.3) | copy-start | bytes 1179652
  784.0 6.4 copy-start.27
  796.9 74.4 %copy-start.8 = (f32[128,1536]{1,0:T(8,128)}, f32[128,1536]{1,0:T(8,128)S(1)}, u32[]{:S(2)}) copy-start(f32[128,1536]{1,0:T(8,128)S(1)} %multiply_add_fusion) | copy-start | bytes 2359300
  905.0 79.0 %reduce-scatter.18.cloned.1.call-start = ((), (), s32[]{:S(2)}) async-start(), calls=%async_computation.12 | async-start | bytes 1769472
  906.9 196.9 %reduce-scatter.20.cloned.1.call-start = ((), (), s32[]{:S(2)}) async-start(), calls=%async_computation.13 | async-start | bytes 811008
  988.5 366.5 %reduce-scatter.12.cloned.1.call-start = ((), (), s32[]{:S(2)}) async-start(), calls=%async_computation.9 | async-start | bytes 29196288 | tf_op jit(solution)/shard_map/reduce_scatter | solution.py:362
  1008.8 12.5 copy-start.28
  1008.8 1006.4 %reduce-scatter.14.cloned.1.call-start = ((), (), s32[]{:S(2)}) async-start(), calls=%async_computation.10 | async-start | bytes 77856768 | tf_op jit(solution)/shard_map/reduce_scatter | solution.py:363
  1021.4 10.2 copy-start.25
  1021.4 10.2 copy-start.26
  1094.3 8.3 copy-start.30
  1094.3 10.3 copy-start.35
  1094.3 260.7 %copy-start.16 = (f32[144,1536]{1,0:T(8,128)S(1)}, f32[144,1536]{1,0:T(8,128)}, u32[]{:S(2)}) copy-start(f32[144,1536]{1,0:T(8,128)} %param.16) | copy-start | bytes 2654212
  1104.6 255.0 %copy-start.34 = (f32[2,48]{1,0:T(2,128)}, f32[2,48]{1,0:T(2,128)S(1)}, u32[]{:S(2)}) copy-start(f32[2,48]{1,0:T(2,128)S(1)} %copy.64) | copy-start | bytes 1156
  1106.5 908.8 %copy-start.7 = (f32[384,1536]{1,0:T(8,128)S(1)}, f32[384,1536]{1,0:T(8,128)}, u32[]{:S(2)}) copy-start(f32[384,1536]{1,0:T(8,128)} %param.17) | copy-start | bytes 7077892
  (26 other events, 84.7 us)
Sparse Core Ops, SparseCore 0:
  489.0 26.1 all-gather.7
  517.6 25.7 all-gather.5
  546.9 214.3 all-gather.9
  764.6 100.6 all-gather.11
  905.1 36.7 reduce-scatter.15
  945.7 38.3 reduce-scatter.17
  989.7 96.2 reduce-scatter.19
  1093.0 261.9 reduce-scatter.11
  1362.0 653.2 reduce-scatter.13
